TPU v7x, 32 devices: a whole 2x2x4 slice. The times are simulated.
32 devices in a mesh: ep: 4 (over y, x), fsdp: 8 (over z, core).
Axes of the slice: x: 2, y: 2, z: 4, core: 2. Of those that a mesh axis runs over, the one named last changes fastest.
Arguments:
- master_down: float32 [16, 6400, 4096], P('ep', None, 'fsdp'), may hold values from -0.109375 to 0.109375
- second_down: bfloat16 [16, 6400, 4096], P('ep', None, 'fsdp'), may hold values from -0.0390625 to 0.0390625
- router_weight: float32 [4096, 16], P('fsdp', 'ep'), may hold values from -0.09375 to 0.09375
- router_gain: float32 [4096], P('fsdp'), may hold values from 0.25 to 1.75
Outputs:
- final_down: bfloat16 [16, 6400, 4096], P('ep', 'fsdp')
- scale_down: float32 [16, 6400], P('ep', 'fsdp')
- serve_router: bfloat16 [4096, 16], replicated
All inputs are finite; a program needn't handle non-finite values. Where the computation divides by a largest or mean magnitude, that divisor is 1e-20 or more.
Results may differ from a plain program's by a relative error of at most 0.001.
Values may be sent and summed in bfloat16 or wider, within the bound.
A program may use at most 256 MiB of HBM per device.

v0:
```python
import jax
import jax.numpy as jnp
from jax import lax
from jax.sharding import PartitionSpec as P


def on_device(master_down, second_down, router_weight, router_gain):
    merged_down = master_down + second_down.astype(jnp.float32)
    scale_down = lax.pmax(jnp.max(jnp.abs(merged_down), axis=2), "fsdp")
    narrow_down = (merged_down / jnp.expand_dims(scale_down, 2)).astype(jnp.bfloat16)
    final_down = lax.all_to_all(narrow_down, "fsdp", split_axis=1, concat_axis=2, tiled=True)
    scale_down = lax.dynamic_slice_in_dim(
        scale_down, lax.axis_index("fsdp") * final_down.shape[1], final_down.shape[1], axis=1
    )
    part_router = (router_weight * router_gain[:, None]).astype(jnp.bfloat16)
    row_router = lax.all_gather(part_router, "fsdp", axis=0, tiled=True)
    serve_router = lax.all_gather(row_router, "ep", axis=1, tiled=True)
    return (final_down, scale_down, serve_router)


def solution(mesh):
    placed = (P("ep", None, "fsdp"), P("ep", None, "fsdp"), P("fsdp", "ep"), P("fsdp"))
    return jax.shard_map(
        on_device,
        mesh=mesh,
        in_specs=placed,
        out_specs=(P("ep", "fsdp", None), P("ep", "fsdp"), P()),
        check_vma=False,
    )
```

profile of v0, /device:TPU:0, one launch (start us, length us, event | category | flops | bytes accessed | tf_op | source)
XLA Modules:
  0.0 839.7 jit_solution(15545822426802912631)
XLA Ops:
  7.2 0.0 all-reduce.2.cloned.1.call-start
  7.2 24.2 %abs_reduce_fusion = f32[4,6400]{1,0:T(4,128)S(1)} fusion(f32[4,6400,512]{2,1,0:T(8,128)} %param.4, bf16[4,6400,512]{2,1,0:T(8,128)(2,1)} %param.5), kind=kLoop, calls=%fused_computation.1 | loop fusion | flops 52403200 | bytes 78745600 | tf_op jit(solution)/shard_map/reduce_max | solution.py:9
  31.4 2.3 copy.21
  33.7 0.0 all-reduce.2.cloned.1.call-update
  33.7 82.1 %all-reduce.2.cloned.1.call-done = f32[4,6400]{0,1:T(8,128)} async-done(((f32[4,6400]{0,1:T(8,128)}), f32[4,6400]{0,1:T(8,128)}) %all-reduce.2.cloned.1.call-update) | async-done | bytes 102416 | tf_op jit(solution)/shard_map/pmax | solution.py:9
  115.8 2.4 copy.17
  118.3 34.3 %divide_convert_fusion = bf16[4,6400,512]{2,1,0:T(8,128)(2,1)} fusion(f32[4,6400,512]{2,1,0:T(8,128)} %param.4, bf16[4,6400,512]{2,1,0:T(8,128)(2,1)} %param.5, f32[4,6400]{1,0:T(4,128)S(1)} %copy.17), kind=kLoop, calls=%fused_computation | loop fusion | flops 52428800 | bytes 104960000 | tf_op jit(solution)/shard_map/convert_element_type | solution.py:10
  152.6 33.4 %copy.18 = bf16[4,6400,512]{2,0,1:T(4,128)(2,1)} copy(bf16[4,6400,512]{2,1,0:T(8,128)(2,1)} %divide_convert_fusion) | data formatting | bytes 52428800 | tf_op jit(solution)/shard_map/convert_element_type | solution.py:10
  185.9 0.0 copy-start
  185.9 0.0 copy-start.1
  185.9 6.6 all-to-all-start
  192.6 0.0 copy-done
  192.6 0.0 copy-done.1
  192.6 571.9 %all_gather.6 = bf16[4096,4]{0,1:T(4,128)(2,1)S(1)} all-gather(bf16[512,4]{0,1:T(4,128)(2,1)S(1)} %multiply_convert_fusion), channel_id=1, replica_groups=mesh['ep'=4,'fsdp'=8] {'fsdp'}, dimensions={0}, use_global_device_ids=true | all-gather | bytes 36864 | tf_op jit(solution)/shard_map/all_gather | solution.py:16
  764.5 8.4 %all-gather = bf16[4,4,4096]{2,1,0:T(4,128)(2,1)S(1)} all-gather(bf16[1,4,4096]{2,1,0:T(4,128)(2,1)S(1)} %bitcast.9), channel_id=1, replica_groups=mesh['ep'=4,'fsdp'=8] {'ep'}, dimensions={0}, use_global_device_ids=true | all-gather | bytes 163840 | tf_op jit(solution)/shard_map/all_gather | solution.py:17
  772.9 0.7 reshape.9
  773.6 1.0 constant_dynamic-slice_fusion
  774.6 0.8 copy.20
  775.4 0.0 all-to-all-done
  775.4 18.2 %copy.19 = bf16[4,800,8,512]{3,2,1,0:T(8,128)(2,1)} copy(bf16[4,800,8,512]{3,0,1,2:T(4,128)(2,1)} %bitcast.1) | data formatting | bytes 52428800 | tf_op jit(solution)/shard_map/all_to_all | solution.py:11
  793.7 39.2 %all_to_all.16 = bf16[4,800,4096]{2,1,0:T(8,128)(2,1)} reshape(bf16[4,800,8,512]{3,2,1,0:T(8,128)(2,1)} %copy.19) | data formatting | bytes 52428800 | tf_op jit(solution)/shard_map/all_to_all | solution.py:11
  (1 shorter events, 0.0 us)
Async XLA Ops:
  7.2 108.7 %all-reduce.2.cloned.1.call-start = ((), (), s32[]{:S(2)}) async-start(), calls=%async_computation.1 | async-start | bytes 6553600 | tf_op jit(solution)/shard_map/pmax | solution.py:9
  185.9 6.7 copy-start
  185.9 6.7 copy-start.1
  185.9 589.5 %all-to-all-start = ((bf16[4,6400,512]{2,0,1:T(4,128)(2,1)}), bf16[4,6400,512]{2,0,1:T(4,128)(2,1)}, u32[]{:S(2)}, u32[]{:S(2)}) async-start(bf16[4,6400,512]{2,0,1:T(4,128)(2,1)} %copy.18), calls=%async_computation | async-start | bytes 52428800 | tf_op jit(solution)/shard_map/all_to_all | solution.py:11
Sparse Core Ops, SparseCore 0:
  33.9 81.9 all-reduce.1
where the time goes:
time: 841 us; the launch traced here: 840 us
  blocking collectives  580 us (69%)
  local copies, waits for them, and re-layouts  98 us (12%)
  waiting for transfers between devices  82.1 us (10%)
  other arithmetic  58.5 us (7%)
  between operations  14.1 us (2%)
    all_gather x1, blocking collectives, on_device(): row_router = lax.all_gather(part_router, 'fsdp', axis=0, tiled=True)  572 us
    pmax x1, waiting for transfers between devices, on_device(): scale_down = lax.pmax(jnp.max(jnp.abs(merged_down), axis=2), 'fsdp')  82.1 us
    all_to_all x2, local copies, waits for them, and re-layouts, on_device(): lax.all_to_all(narrow_down, 'fsdp', split_axis=1, concat_axis=2, tiled=True)  57.4 us
    convert_element_type x1, other arithmetic, on_device(): (merged_down / jnp.expand_dims(scale_down, 2)).astype(jnp.bfloat16)  34.3 us
    convert_element_type x1, local copies, waits for them, and re-layouts, on_device(): (merged_down / jnp.expand_dims(scale_down, 2)).astype(jnp.bfloat16)  33.4 us
    reduce_max x1, other arithmetic, on_device(): scale_down = lax.pmax(jnp.max(jnp.abs(merged_down), axis=2), 'fsdp')  24.2 us
  transfers between devices with their start and end apart: 2, of which 1 were waited for; matrix products, arithmetic and copies ran while one was open for 0% of the time, Pallas kernels for 0%

commit v1 on v0

--- a/solution.py
+++ b/solution.py
@@ -8,7 +8,12 @@
     merged_down = master_down + second_down.astype(jnp.float32)
     scale_down = lax.pmax(jnp.max(jnp.abs(merged_down), axis=2), "fsdp")
     narrow_down = (merged_down / jnp.expand_dims(scale_down, 2)).astype(jnp.bfloat16)
-    final_down = lax.all_to_all(narrow_down, "fsdp", split_axis=1, concat_axis=2, tiled=True)
+    final_down = jnp.concatenate(
+        lax.all_to_all(
+            jnp.stack(jnp.split(narrow_down, lax.axis_size("fsdp"), axis=1)), "fsdp", 0, 0
+        ),
+        axis=2,
+    )
     scale_down = lax.dynamic_slice_in_dim(
         scale_down, lax.axis_index("fsdp") * final_down.shape[1], final_down.shape[1], axis=1
     )

time: 841 us -> 767 us (0.912)
  local copies, waits for them, and re-layouts: 98 us -> 50.6 us
  waiting for transfers between devices: 82.1 us -> 55.3 us
    all_to_all x2 -> x0, local copies, waits for them, and re-layouts: 57.4 us -> none  [on_device(): lax.all_to_all(narrow_down, 'fsdp', split_axis=1, concat_axis=2, tiled=True)]
    convert_element_type x1 -> x0, local copies, waits for them, and re-layouts: 33.4 us -> none  [on_device(): (merged_down / jnp.expand_dims(scale_down, 2)).astype(jnp.bfloat16)]
    pmax x1, waiting for transfers between devices: 82.1 us -> 55.3 us  [on_device(): scale_down = lax.pmax(jnp.max(jnp.abs(merged_down), axis=2), 'fsdp')]
    unnamed x7 -> x12, local copies, waits for them, and re-layouts: 3.75 us -> 27.5 us
    reshape x0 -> x1, local copies, waits for them, and re-layouts: none -> 17.9 us  [on_device(): jnp.concatenate(lax.all_to_all(jnp.stack(jnp.split(narrow_down, lax.axis_...]
where the time goes in v1:
time: 767 us; the launch traced here: 766 us
  blocking collectives  580 us (76%)
  other arithmetic  59.2 us (8%)
  waiting for transfers between devices  55.3 us (7%)
  local copies, waits for them, and re-layouts  50.6 us (7%)
  between operations  14.1 us (2%)
    all_gather x1, blocking collectives, on_device(): row_router = lax.all_gather(part_router, 'fsdp', axis=0, tiled=True)  572 us
    pmax x1, waiting for transfers between devices, on_device(): scale_down = lax.pmax(jnp.max(jnp.abs(merged_down), axis=2), 'fsdp')  55.3 us
    convert_element_type x1, other arithmetic, on_device(): (merged_down / jnp.expand_dims(scale_down, 2)).astype(jnp.bfloat16)  34.4 us
    unnamed x12, local copies, waits for them, and re-layouts  27.5 us
    reduce_max x1, other arithmetic, on_device(): scale_down = lax.pmax(jnp.max(jnp.abs(merged_down), axis=2), 'fsdp')  24.9 us
    reshape x1, local copies, waits for them, and re-layouts, on_device(): jnp.concatenate(lax.all_to_all(jnp.stack(jnp.split(narrow_down, lax.axis_...  17.9 us
  transfers between devices with their start and end apart: 2, of which 1 were waited for; matrix products, arithmetic and copies ran while one was open for 0% of the time, Pallas kernels for 0%

profile of v1, /device:TPU:0, one launch (start us, length us, event | category | flops | bytes accessed | tf_op | source)
XLA Modules:
  0.0 766.2 jit_solution(10804507981940321855)
XLA Ops:
  7.2 0.0 all-reduce.2.cloned.1.call-start
  7.2 24.9 %abs_reduce_fusion = f32[4,6400]{1,0:T(4,128)} fusion(f32[4,6400,512]{2,1,0:T(8,128)} %param.4, bf16[4,6400,512]{2,1,0:T(8,128)(2,1)} %param.5), kind=kLoop, calls=%fused_computation.1 | loop fusion | flops 52403200 | bytes 78745600 | tf_op jit(solution)/shard_map/reduce_max | solution.py:9
  32.1 0.0 all-reduce.2.cloned.1.call-update
  32.1 55.3 %all-reduce.2.cloned.1.call-done = f32[4,6400]{1,0:T(4,128)} async-done(((f32[4,6400]{1,0:T(4,128)}), f32[4,6400]{1,0:T(4,128)}) %all-reduce.2.cloned.1.call-update) | async-done | bytes 102416 | tf_op jit(solution)/shard_map/pmax | solution.py:9
  87.4 34.4 %divide_convert_fusion = bf16[4,6400,512]{2,1,0:T(8,128)(2,1)} fusion(f32[4,6400,512]{2,1,0:T(8,128)} %param.4, bf16[4,6400,512]{2,1,0:T(8,128)(2,1)} %param.5, f32[4,6400]{1,0:T(4,128)} %all-reduce.2.cloned.1.call-done), kind=kLoop, calls=%fused_computation | loop fusion | flops 52428800 | bytes 104960000 | tf_op jit(solution)/shard_map/convert_element_type | solution.py:10
  121.8 3.8 fusion.7
  125.6 3.8 fusion.6
  129.5 3.8 fusion.5
  133.2 3.8 fusion.4
  137.1 3.9 fusion.3
  141.0 3.8 fusion.2
  144.8 3.8 fusion.1
  148.6 3.8 fusion
  152.4 0.0 copy-start
  152.4 0.0 copy-start.1
  152.4 6.6 all-to-all-start
  159.1 0.0 copy-done
  159.1 0.0 copy-done.1
  159.1 571.9 %all_gather.6 = bf16[4096,4]{0,1:T(4,128)(2,1)S(1)} all-gather(bf16[512,4]{0,1:T(4,128)(2,1)S(1)} %multiply_convert_fusion), channel_id=1, replica_groups=mesh['ep'=4,'fsdp'=8] {'fsdp'}, dimensions={0}, use_global_device_ids=true | all-gather | bytes 36864 | tf_op jit(solution)/shard_map/all_gather | solution.py:21
  731.0 8.4 %all-gather = bf16[4,4,4096]{2,1,0:T(4,128)(2,1)S(1)} all-gather(bf16[1,4,4096]{2,1,0:T(4,128)(2,1)S(1)} %bitcast.40), channel_id=1, replica_groups=mesh['ep'=4,'fsdp'=8] {'ep'}, dimensions={0}, use_global_device_ids=true | all-gather | bytes 163840 | tf_op jit(solution)/shard_map/all_gather | solution.py:22
  739.4 0.7 reshape.17
  740.1 1.4 constant_dynamic-slice_fusion
  741.5 0.0 all-to-all-done
  741.5 17.9 %copy.9 = bf16[8,4,100,8,512]{4,3,0,2,1:T(8,128)(2,1)} copy(bf16[8,4,100,8,512]{4,3,2,1,0:T(8,128)(2,1)} %bitcast.13) | data formatting | bytes 52428800 | tf_op jit(solution)/shard_map/reshape | solution.py:11
  (1 shorter events, 0.0 us)
Async XLA Ops:
  7.2 80.3 %all-reduce.2.cloned.1.call-start = ((), (), s32[]{:S(2)}) async-start(), calls=%async_computation.1 | async-start | bytes 204800 | tf_op jit(solution)/shard_map/pmax | solution.py:9
  152.4 6.6 copy-start
  152.4 6.6 copy-start.1
  152.4 589.1 %all-to-all-start = ((bf16[8,4,800,512]{3,2,1,0:T(8,128)(2,1)}), bf16[8,4,800,512]{3,2,1,0:T(8,128)(2,1)}, u32[]{:S(2)}, u32[]{:S(2)}) async-start(bf16[8,4,800,512]{3,2,1,0:T(8,128)(2,1)} %fusion), calls=%async_computation | async-start | bytes 52428800 | tf_op jit(solution)/shard_map/all_to_all | solution.py:12
Sparse Core Ops, SparseCore 0:
  32.2 55.1 all-reduce.1
